TPU v7x, 32 devices: a whole 2x2x4 slice. The times are simulated.
32 devices in a mesh: row: 4 (over y, x), col: 8 (over z, core).
Axes of the slice: x: 2, y: 2, z: 4, core: 2. Of those that a mesh axis runs over, the one named last changes fastest.
Arguments:
- psi: bfloat16 [8192, 8192], P(('row', 'col')), may hold values from -0.125 to 0.125
- hpsi: bfloat16 [8192, 128], P(('row', 'col')), may hold values from -0.796875 to 0.796875
- slab_counts: int32 [32], P(('row', 'col')), may hold values from 1 to 256, 6144 in all
- matrix: float32 [4, 2048, 8, 1024], P('row', None, 'col'), as said below
Outputs:
- reduced: float32 [4, 2048, 8, 1024], P('row', None, 'col')
Inputs may be any that keep to these rules, and one draw needn't show every extreme that they name: Slab k's live plane waves are its first slab_counts[k] slots; the rest are padding; the counts sum to 3 * 256 * 32 // 4. The stored matrix is symmetric.
All inputs are finite; a program needn't handle non-finite values.
Results may differ from a plain program's by a relative error of at most 0.0003.
Values sent between devices are 32-bit elements; how exact they have to be, the bound alone decides.
No kernel may reach another device: no remote copies, remote signals or barrier semaphores. Data moves between devices by JAX's collectives and lax.ppermute only.
A program may use at most 64 MiB of HBM per device.

v0:
```python
import jax
import jax.numpy as jnp
from jax import lax
from jax.sharding import PartitionSpec as P

TILE = 16
HIGH = lax.Precision.HIGHEST


def lower_solve(factor, rhs):
    return lax.linalg.triangular_solve(factor, rhs, left_side=True, lower=True)


def invert_shifted(shifted):
    normal = jnp.dot(shifted.T, shifted, precision=HIGH)
    factor = jnp.linalg.cholesky(normal)
    first = lower_solve(factor, shifted.T)
    return lax.linalg.triangular_solve(factor, first, left_side=True, lower=True, transpose_a=True)


def per_device(psi, hpsi, slab_counts, matrix):
    prow_id = lax.axis_index("row")
    pcol_id = lax.axis_index("col")
    n_row = lax.axis_size("row")
    n_col = lax.axis_size("col")
    slots = psi.shape[0]
    panel = hpsi.shape[1]
    local_rows = matrix.shape[1]
    local_cols = matrix.shape[3]
    tiles_r = local_rows // TILE
    tiles_c = local_cols // TILE
    valid = jnp.arange(slots, dtype=jnp.int32) < slab_counts[0]
    hcols = jnp.where(valid[:, None], hpsi, jnp.zeros_like(hpsi))
    local_r = jnp.arange(local_rows, dtype=jnp.int32)
    local_c = jnp.arange(local_cols, dtype=jnp.int32)
    row_global = (local_r // TILE * n_row + prow_id) * TILE + local_r % TILE
    col_global = (local_c // TILE * n_col + pcol_id) * TILE + local_c % TILE
    partial_value = lax.dot_general(
        psi, hcols, (((0,), (0,)), ((), ())), preferred_element_type=jnp.float32
    )
    whole = lax.psum(partial_value, ("row", "col"))
    prow = lax.dynamic_index_in_dim(
        whole.reshape(tiles_r, n_row, TILE, panel), prow_id, 1, keepdims=False
    ).reshape(local_rows, panel)
    scols = lax.dynamic_index_in_dim(
        whole.reshape(tiles_c, n_col, TILE, panel), pcol_id, 1, keepdims=False
    ).reshape(local_cols, panel)
    span = jnp.arange(panel, dtype=jnp.int32)
    lower_r = jnp.where((row_global >= panel)[:, None], prow, jnp.zeros_like(prow))
    lower_c = jnp.where((col_global >= panel)[:, None], scols, jnp.zeros_like(scols))
    top_select = (row_global[None, :] == panel + span[:, None]).astype(jnp.float32)
    gram_part = jnp.dot(lower_r.T, lower_r, precision=HIGH)
    top_part = jnp.dot(top_select, prow, precision=HIGH)
    gram, top_rows = lax.psum((gram_part, top_part), "row")
    factor = jnp.linalg.cholesky(gram)
    basis_r = lower_solve(factor, lower_r.T).T
    basis_c = lower_solve(factor, lower_c.T).T
    top = lower_solve(factor, top_rows.T).T
    inverse = invert_shifted(jnp.eye(panel, dtype=jnp.float32) - top)
    embed_r = (row_global[:, None] == panel + span[None, :]).astype(jnp.float32)
    embed_c = (col_global[:, None] == panel + span[None, :]).astype(jnp.float32)
    reflect_r = basis_r - embed_r
    reflect_c = basis_c - embed_c
    stored = matrix[0, :, 0, :]
    col_select = (col_global[None, :] == span[:, None]).astype(jnp.float32)
    row_select = (row_global[None, :] == span[:, None]).astype(jnp.float32)
    left = jnp.dot(prow, col_select, precision=HIGH)
    upper = lax.dot_general(row_select, scols, (((0,), (1,)), ((), ())), precision=HIGH)
    inside_r = (row_global < panel)[:, None]
    inside_c = (col_global < panel)[None, :]
    refreshed = jnp.where(
        inside_r & inside_c,
        0.5 * (left + upper),
        jnp.where(inside_c, left, jnp.where(inside_r, upper, stored)),
    )
    zpart = jnp.dot(refreshed, reflect_c, precision=HIGH)
    zrows = lax.psum(zpart, "col")
    upart = lax.dot_general(refreshed, reflect_r, (((0,), (0,)), ((), ())), precision=HIGH)
    ucols = lax.psum(upart, "row")
    wmat = lax.psum(jnp.dot(reflect_r.T, zrows, precision=HIGH), "row")
    core = jnp.dot(jnp.dot(inverse, wmat, precision=HIGH), inverse.T, precision=HIGH)
    first = jnp.dot(reflect_r, jnp.dot(inverse, ucols.T, precision=HIGH), precision=HIGH)
    second = jnp.dot(
        jnp.dot(zrows, inverse.T, precision=HIGH) - jnp.dot(reflect_r, core, precision=HIGH),
        reflect_c.T,
        precision=HIGH,
    )
    return (refreshed - first - second)[None, :, None, :]


def solution(mesh):
    in_specs = (
        P(("row", "col"), None),
        P(("row", "col"), None),
        P(("row", "col")),
        P("row", None, "col", None),
    )
    out_specs = P("row", None, "col", None)
    return jax.shard_map(
        per_device, mesh=mesh, in_specs=in_specs, out_specs=out_specs, check_vma=False
    )
```

profile of v0, /device:TPU:0, one launch (start us, length us, event | category | flops | bytes accessed | tf_op | source)
XLA Modules:
  0.0 421.6 jit_solution(14257435263756658271)
XLA Ops:
  7.2 5.1 %convolution_bitcast_fusion = f32[8192,128]{0,1:T(8,128)} fusion(bf16[256,8192]{1,0:T(8,128)(2,1)} %param.7, bf16[256,128]{1,0:T(8,128)(2,1)} %param.8, pred[256]{0:T(512)(128)(4,1)S(1)} %iota_compare_fusion.9), kind=kOutput, calls=%fused_computation | convolution fusion | flops 536903680 | bytes 8454400 | tf_op jit(solution)/shard_map/dot_general | solution.py:38
  12.3 0.0 all-reduce.6.cloned.1.call-update
  12.3 0.0 all-reduce.8.cloned.1.call-start
  12.5 0.1 fusion.18
  12.6 145.3 %all-reduce.6.cloned.1.call-done = f32[8192,128]{0,1:T(8,128)} async-done(((f32[8192,128]{0,1:T(8,128)}), f32[8192,128]{0,1:T(8,128)}) %all-reduce.6.cloned.1.call-update) | async-done | bytes 4194320 | tf_op jit(solution)/shard_map/psum | solution.py:41
  157.9 5.6 %copy.11 = f32[8192,128]{1,0:T(8,128)} copy(f32[8192,128]{0,1:T(8,128)} %all-reduce.6.cloned.1.call-done) | data formatting | bytes 8388608 | tf_op jit(solution)/shard_map/psum | solution.py:41
  163.4 1.6 broadcast_select_fusion
  165.0 2.4 convolution_bitcast_fusion.1
  167.5 0.0 all-reduce.8.cloned.1.call-update
  167.5 0.0 all-reduce.10.cloned.1.call-start
  167.5 3.6 fusion.10
  171.1 1.3 broadcast_select_fusion.1
  172.4 11.0 %fusion.1 = f32[2048,1024]{1,0:T(8,128)} fusion(f32[2048,1024]{1,0:T(8,128)S(1)} %fusion.10, f32[1,2048,1,1024]{3,2,1,0:T(1,128)} %param.10, pred[1024]{0:T(1024)(128)(4,1)S(1)} %broadcast_compare_fusion.1, pred[2048]{0:T(1024)(128)(4,1)S(1)} %broadcast_compare_fusion, f32[1024,128]{1,0:T(8,128)S(1)} %bitcast.89, s32[2048]{0:T(1024)S(1)} %fusion.60), kind=kOutput, calls=%fused_computation.3 | convolution fusion | flops 3234332672 | bytes 25701376 | tf_op jit(solution)/shard_map/dot_general | solution.py:68
  183.3 1.6 fusion.4
  185.0 23.8 %all-reduce.8.cloned.1.call-done = f32[128,128]{0,1:T(8,128)} async-done(((f32[128,128]{0,1:T(8,128)}), f32[128,128]{0,1:T(8,128)}) %all-reduce.8.cloned.1.call-update) | async-done | bytes 65552 | tf_op jit(solution)/shard_map/psum | solution.py:54
  208.8 0.9 copy.16
  209.7 0.9 fusion.29
  210.5 11.7 %cholesky.44 = f32[128,128]{1,0:T(8,128)S(1)} custom-call(f32[128,128]{1,0:T(8,128)S(1)} %fusion.29), custom_call_target="Cholesky" | custom-call | tf_op jit(solution)/shard_map/jit(cholesky)/cholesky | solution.py:55
  222.3 0.7 compare_reduce_fusion.1
  223.0 0.7 fusion.12
  223.7 9.8 %custom-call.13 = f32[1,128,128]{1,2,0:T(8,128)S(1)} custom-call(f32[1,128,128]{2,1,0:T(8,128)S(1)} %fusion.12), custom_call_target="InvertDiagBlocksLowerTriangular" | custom-call | tf_op jit(solution)/shard_map/triangular_solve | solution.py:11
  233.5 0.6 convolution_subtract_fusion.2
  234.1 10.1 %fusion.77 = f32[2048,128]{1,0:T(8,128)} fusion(f32[2048,1024]{1,0:T(8,128)} %fusion.1, f32[1024,128]{1,0:T(8,128)S(1)} %convolution_subtract_fusion.2), kind=kOutput, calls=%fused_computation.122 | convolution fusion | flops 3221225472 | bytes 9961472 | tf_op jit(solution)/shard_map/dot_general | solution.py:76
  244.2 0.0 all-reduce.10.cloned.1.call-update
  244.2 0.0 all-reduce.12.cloned.1.call-start
  244.2 1.0 convolution_subtract_fusion.1
  245.2 16.6 %fusion.74 = f32[1024,128]{1,0:T(8,128)} fusion(f32[2048,1024]{1,0:T(8,128)} %fusion.1, f32[2048,128]{1,0:T(8,128)S(1)} %convolution_subtract_fusion.1), kind=kOutput, calls=%fused_computation.119 | convolution fusion | flops 3221225472 | bytes 9961472 | tf_op jit(solution)/shard_map/dot_general | solution.py:78
  261.8 41.8 %all-reduce.10.cloned.1.call-done = f32[2048,128]{1,0:T(8,128)} async-done(((f32[2048,128]{1,0:T(8,128)}), f32[2048,128]{1,0:T(8,128)}) %all-reduce.10.cloned.1.call-update) | async-done | bytes 1048592 | tf_op jit(solution)/shard_map/psum | solution.py:77
  303.7 3.7 fusion.79
  307.3 0.0 all-reduce.12.cloned.1.call-update
  307.3 46.2 %all-reduce.12.cloned.1.call-done = (f32[128,128]{1,0:T(8,128)}, f32[1024,128]{1,0:T(8,128)}, f32[128,128]{1,0:T(8,128)}) async-done(((f32[128,128]{1,0:T(8,128)}, f32[1024,128]{1,0:T(8,128)}, f32[128,128]{1,0:T(8,128)}), (f32[128,128]{1,0:T(8,128)}, f32[1024,128]{1,0:T(8,128)}, f32[128,128]{1,0:T(8,128)})) %all-reduce.12.cloned.1.call-update) | async-done | bytes 655376 | tf_op jit(solution)/shard_map/psum | solution.py:54
  353.6 1.1 fusion.25
  354.7 0.3 fusion.24
  355.0 0.1 copy.17
  355.1 11.7 %cholesky.55 = f32[128,128]{1,0:T(8,128)S(1)} custom-call(f32[128,128]{1,0:T(8,128)S(1)} %fusion.23), custom_call_target="Cholesky" | custom-call | tf_op jit(solution)/shard_map/jit(cholesky)/cholesky | solution.py:16
  366.8 0.6 compare_reduce_fusion
  367.4 0.6 fusion.13
  368.0 9.8 %custom-call.14 = f32[1,128,128]{1,2,0:T(8,128)S(1)} custom-call(f32[1,128,128]{2,1,0:T(8,128)S(1)} %fusion.13), custom_call_target="InvertDiagBlocksLowerTriangular" | custom-call | tf_op jit(solution)/shard_map/triangular_solve | solution.py:18
  377.8 0.3 fusion.19
  378.1 0.2 fusion.21
  378.3 1.0 fusion.80
  379.4 0.3 fusion.81
  379.7 1.8 fusion.75
  381.4 7.2 %fusion.76 = f32[2048,1024]{1,0:T(8,128)S(1)} fusion(f32[2048,128]{1,0:T(8,128)S(1)} %convolution_subtract_fusion.1, f32[128,1024]{1,0:T(8,128)S(1)} %fusion.75), kind=kOutput, calls=%fused_computation.121 | convolution fusion | flops 3221225472 | bytes 9961472 | tf_op jit(solution)/shard_map/dot_general | solution.py:82
  388.7 1.0 fusion.78
  389.7 1.0 convolution_subtract_fusion
  390.7 8.0 %subtract_bitcast_fusion = f32[1,2048,1,1024]{3,1,2,0:T(8,128)S(1)} fusion(f32[2048,1024]{1,0:T(8,128)S(1)} %bitcast.83, f32[2048,1024]{1,0:T(8,128)S(1)} %fusion.76, f32[2048,128]{1,0:T(8,128)S(1)} %convolution_subtract_fusion, f32[1024,128]{1,0:T(8,128)S(1)} %convolution_subtract_fusion.2), kind=kOutput, calls=%fused_computation.4 | convolution fusion | flops 3225419776 | bytes 26738688 | tf_op jit(solution)/shard_map/dot_general | solution.py:83
  398.7 16.1 %copy.18 = f32[1,2048,1,1024]{3,2,1,0:T(1,128)} copy(f32[1,2048,1,1024]{3,1,2,0:T(8,128)S(1)} %subtract_bitcast_fusion) | data formatting | bytes 16777216 | tf_op jit(solution)/shard_map/broadcast_in_dim | solution.py:88
  (18 shorter events, 0.2 us)
Async XLA Ops:
  6.5 151.3 %all-reduce.6.cloned.1.call-start = ((), (), s32[]{:S(2)}) async-start(), calls=%async_computation | async-start | bytes 8388608 | tf_op jit(solution)/shard_map/psum | solution.py:41
  12.3 196.4 %all-reduce.8.cloned.1.call-start = ((), (), s32[]{:S(2)}) async-start(), calls=%async_computation.1 | async-start | bytes 131072 | tf_op jit(solution)/shard_map/psum | solution.py:54
  167.5 136.2 %all-reduce.10.cloned.1.call-start = ((), (), s32[]{:S(2)}) async-start(), calls=%async_computation.2 | async-start | bytes 2097152 | tf_op jit(solution)/shard_map/psum | solution.py:77
  244.2 109.4 %all-reduce.12.cloned.1.call-start = ((), (), s32[]{:S(2)}) async-start(), calls=%async_computation.3 | async-start | bytes 1310720 | tf_op jit(solution)/shard_map/psum | solution.py:54
  379.6 9.0 %copy-start = (f32[2048,128]{1,0:T(8,128)S(1)}, f32[2048,128]{1,0:T(8,128)}, u32[]{:S(2)}) copy-start(f32[2048,128]{1,0:T(8,128)} %all-reduce.10.cloned.1.call-done) | copy-start | bytes 3145732
  379.6 11.0 %slice-start = ((s8[8388608]{0:T(1024)(128)(4,1)}), s8[4194304]{0:T(1024)(128)(4,1)S(1)}, s32[]{:S(2)}) async-start(s8[8388608]{0:T(1024)(128)(4,1)} %bitcast.82), calls=%async_computation.4 | async-start | bytes 8388608
  381.4 9.3 %slice-start.1 = ((s8[8388608]{0:T(1024)(128)(4,1)}), s8[4194304]{0:T(1024)(128)(4,1)S(1)}, s32[]{:S(2)}) async-start(s8[8388608]{0:T(1024)(128)(4,1)} %bitcast.82), calls=%async_computation.5 | async-start | bytes 8388608
Sparse Core Ops, SparseCore 0:
  12.9 144.9 all-reduce.5
  167.6 41.1 all-reduce.7
  244.3 59.2 all-reduce.9
  307.5 46.0 all-reduce.11
where the time goes:
time: 428 us; the launch traced here: 422 us
  waiting for transfers between devices  257 us (60%)
  matrix products  77.7 us (18%)
  other arithmetic  49.6 us (12%)
  local copies, waits for them, and re-layouts  22.7 us (5%)
  between operations  14.3 us (3%)
    psum x1, waiting for transfers between devices, per_device(): whole = lax.psum(partial_value, ('row', 'col'))  145 us
    psum x2, waiting for transfers between devices, per_device(): gram, top_rows = lax.psum((gram_part, top_part), 'row')  70 us
    psum x1, waiting for transfers between devices, per_device(): zrows = lax.psum(zpart, 'col')  41.8 us
    dot_general x1, matrix products, per_device(): lax.dot_general(refreshed, reflect_r, (((0,), (0,)), ((), ())), precision...  16.6 us
    broadcast_in_dim x1, local copies, waits for them, and re-layouts, per_device(): return (refreshed - first - second)[None, :, None, :]  16.1 us
    another operation x3, other arithmetic, per_device(): factor = jnp.linalg.cholesky(gram)  12.5 us
    another operation x3, other arithmetic, invert_shifted(): factor = jnp.linalg.cholesky(normal)  12.4 us
    dot_general x1, matrix products, per_device(): lax.dot_general(row_select, scols, (((0,), (1,)), ((), ())), precision=HIGH)  11 us
  transfers between devices with their start and end apart: 4, of which 4 were waited for; matrix products, arithmetic and copies ran while one was open for 8% of the time, Pallas kernels for 0%

commit v1 on v0

--- a/solution.py
+++ b/solution.py
@@ -38,7 +38,9 @@
     partial_value = lax.dot_general(
         psi, hcols, (((0,), (0,)), ((), ())), preferred_element_type=jnp.float32
     )
-    whole = lax.psum(partial_value, ("row", "col"))
+    whole = partial_value
+    for mesh_axis in ("col", "row"):
+        whole = lax.psum(whole, mesh_axis)
     prow = lax.dynamic_index_in_dim(
         whole.reshape(tiles_r, n_row, TILE, panel), prow_id, 1, keepdims=False
     ).reshape(local_rows, panel)

time: 428 us -> 489 us (1.14)
  waiting for transfers between devices: 257 us -> 319 us
    psum x1 -> x2, waiting for transfers between devices: 145 us -> 206 us  [per_device(): whole = lax.psum(whole, mesh_axis)]
  transfers between devices with their start and end apart: 4 -> 5, of which waited for: 4 -> 5; matrix products, arithmetic and copies ran while one was open for 8% -> 7% of each run, Pallas kernels for 0% -> 0%
where the time goes in v1:
time: 489 us; the launch traced here: 483 us
  waiting for transfers between devices  319 us (65%)
  matrix products  77.7 us (16%)
  other arithmetic  49.6 us (10%)
  local copies, waits for them, and re-layouts  22.7 us (5%)
  between operations  14.3 us (3%)
    psum x2, waiting for transfers between devices, per_device(): whole = lax.psum(whole, mesh_axis)  206 us
    psum x2, waiting for transfers between devices, per_device(): gram, top_rows = lax.psum((gram_part, top_part), 'row')  70.7 us
    psum x1, waiting for transfers between devices, per_device(): zrows = lax.psum(zpart, 'col')  41.8 us
    dot_general x1, matrix products, per_device(): lax.dot_general(refreshed, reflect_r, (((0,), (0,)), ((), ())), precision...  16.6 us
    broadcast_in_dim x1, local copies, waits for them, and re-layouts, per_device(): return (refreshed - first - second)[None, :, None, :]  16.1 us
    another operation x3, other arithmetic, per_device(): factor = jnp.linalg.cholesky(gram)  12.5 us
    another operation x3, other arithmetic, invert_shifted(): factor = jnp.linalg.cholesky(normal)  12.4 us
    dot_general x1, matrix products, per_device(): lax.dot_general(row_select, scols, (((0,), (1,)), ((), ())), precision=HIGH)  11 us
  transfers between devices with their start and end apart: 5, of which 5 were waited for; matrix products, arithmetic and copies ran while one was open for 7% of the time, Pallas kernels for 0%

profile of v1, /device:TPU:0, one launch (start us, length us, event | category | flops | bytes accessed | tf_op | source)
XLA Modules:
  0.0 483.0 jit_solution(4359291769788836729)
XLA Ops:
  7.2 5.1 %convolution_bitcast_fusion = f32[8192,128]{0,1:T(8,128)} fusion(bf16[256,8192]{1,0:T(8,128)(2,1)} %param.7, bf16[256,128]{1,0:T(8,128)(2,1)} %param.8, pred[256]{0:T(512)(128)(4,1)S(1)} %iota_compare_fusion.9), kind=kOutput, calls=%fused_computation | convolution fusion | flops 536903680 | bytes 8454400 | tf_op jit(solution)/shard_map/dot_general | solution.py:38
  12.3 0.0 all-reduce.7.cloned.1.call-update
  12.3 0.0 all-reduce.9.cloned.1.call-start
  12.4 99.3 %all-reduce.7.cloned.1.call-done = f32[8192,128]{0,1:T(8,128)} async-done(((f32[8192,128]{0,1:T(8,128)}), f32[8192,128]{0,1:T(8,128)}) %all-reduce.7.cloned.1.call-update) | async-done | bytes 4194320 | tf_op jit(solution)/shard_map/psum | solution.py:43
  111.7 0.0 all-reduce.9.cloned.1.call-update
  111.7 0.0 all-reduce.11.cloned.1.call-start
  111.8 0.1 fusion.18
  111.9 106.7 %all-reduce.9.cloned.1.call-done = f32[8192,128]{0,1:T(8,128)} async-done(((f32[8192,128]{0,1:T(8,128)}), f32[8192,128]{0,1:T(8,128)}) %all-reduce.9.cloned.1.call-update) | async-done | bytes 4194320 | tf_op jit(solution)/shard_map/psum | solution.py:43
  218.6 5.6 %copy.11 = f32[8192,128]{1,0:T(8,128)} copy(f32[8192,128]{0,1:T(8,128)} %all-reduce.9.cloned.1.call-done) | data formatting | bytes 8388608 | tf_op jit(solution)/shard_map/psum | solution.py:43
  224.2 1.6 broadcast_select_fusion
  225.8 2.4 convolution_bitcast_fusion.1
  228.2 0.0 all-reduce.13.cloned.1.call-start
  228.3 3.6 fusion.10
  231.9 1.3 broadcast_select_fusion.1
  233.1 11.0 %fusion.1 = f32[2048,1024]{1,0:T(8,128)} fusion(f32[2048,1024]{1,0:T(8,128)S(1)} %fusion.10, f32[1,2048,1,1024]{3,2,1,0:T(1,128)} %param.10, pred[1024]{0:T(1024)(128)(4,1)S(1)} %broadcast_compare_fusion.1, pred[2048]{0:T(1024)(128)(4,1)S(1)} %broadcast_compare_fusion, f32[1024,128]{1,0:T(8,128)S(1)} %bitcast.89, s32[2048]{0:T(1024)S(1)} %fusion.60), kind=kOutput, calls=%fused_computation.3 | convolution fusion | flops 3234332672 | bytes 25701376 | tf_op jit(solution)/shard_map/dot_general | solution.py:70
  244.1 1.6 fusion.4
  245.8 24.5 %all-reduce.11.cloned.1.call-done = f32[128,128]{0,1:T(8,128)} async-done(((f32[128,128]{0,1:T(8,128)}), f32[128,128]{0,1:T(8,128)}) %all-reduce.11.cloned.1.call-update) | async-done | bytes 65552 | tf_op jit(solution)/shard_map/psum | solution.py:56
  270.2 0.9 copy.16
  271.2 0.9 fusion.29
  272.0 11.7 %cholesky.44 = f32[128,128]{1,0:T(8,128)S(1)} custom-call(f32[128,128]{1,0:T(8,128)S(1)} %fusion.29), custom_call_target="Cholesky" | custom-call | tf_op jit(solution)/shard_map/jit(cholesky)/cholesky | solution.py:57
  283.8 0.7 compare_reduce_fusion.1
  284.5 0.7 fusion.12
  285.2 9.8 %custom-call.13 = f32[1,128,128]{1,2,0:T(8,128)S(1)} custom-call(f32[1,128,128]{2,1,0:T(8,128)S(1)} %fusion.12), custom_call_target="InvertDiagBlocksLowerTriangular" | custom-call | tf_op jit(solution)/shard_map/triangular_solve | solution.py:11
  295.0 0.6 convolution_subtract_fusion.2
  295.6 10.1 %fusion.77 = f32[2048,128]{1,0:T(8,128)} fusion(f32[2048,1024]{1,0:T(8,128)} %fusion.1, f32[1024,128]{1,0:T(8,128)S(1)} %convolution_subtract_fusion.2), kind=kOutput, calls=%fused_computation.122 | convolution fusion | flops 3221225472 | bytes 9961472 | tf_op jit(solution)/shard_map/dot_general | solution.py:78
  305.7 0.0 all-reduce.15.cloned.1.call-start
  305.7 1.0 convolution_subtract_fusion.1
  306.7 16.6 %fusion.74 = f32[1024,128]{1,0:T(8,128)} fusion(f32[2048,1024]{1,0:T(8,128)} %fusion.1, f32[2048,128]{1,0:T(8,128)S(1)} %convolution_subtract_fusion.1), kind=kOutput, calls=%fused_computation.119 | convolution fusion | flops 3221225472 | bytes 9961472 | tf_op jit(solution)/shard_map/dot_general | solution.py:80
  323.3 41.8 %all-reduce.13.cloned.1.call-done = f32[2048,128]{1,0:T(8,128)} async-done(((f32[2048,128]{1,0:T(8,128)}), f32[2048,128]{1,0:T(8,128)}) %all-reduce.13.cloned.1.call-update) | async-done | bytes 1048592 | tf_op jit(solution)/shard_map/psum | solution.py:79
  365.1 3.7 fusion.79
  368.8 46.2 %all-reduce.15.cloned.1.call-done = (f32[128,128]{1,0:T(8,128)}, f32[1024,128]{1,0:T(8,128)}, f32[128,128]{1,0:T(8,128)}) async-done(((f32[128,128]{1,0:T(8,128)}, f32[1024,128]{1,0:T(8,128)}, f32[128,128]{1,0:T(8,128)}), (f32[128,128]{1,0:T(8,128)}, f32[1024,128]{1,0:T(8,128)}, f32[128,128]{1,0:T(8,128)})) %all-reduce.15.cloned.1.call-update) | async-done | bytes 655376 | tf_op jit(solution)/shard_map/psum | solution.py:56
  415.1 1.1 fusion.25
  416.2 0.3 fusion.24
  416.4 0.1 copy.17
  416.6 11.7 %cholesky.55 = f32[128,128]{1,0:T(8,128)S(1)} custom-call(f32[128,128]{1,0:T(8,128)S(1)} %fusion.23), custom_call_target="Cholesky" | custom-call | tf_op jit(solution)/shard_map/jit(cholesky)/cholesky | solution.py:16
  428.3 0.6 compare_reduce_fusion
  428.9 0.6 fusion.13
  429.5 9.8 %custom-call.14 = f32[1,128,128]{1,2,0:T(8,128)S(1)} custom-call(f32[1,128,128]{2,1,0:T(8,128)S(1)} %fusion.13), custom_call_target="InvertDiagBlocksLowerTriangular" | custom-call | tf_op jit(solution)/shard_map/triangular_solve | solution.py:18
  439.3 0.3 fusion.19
  439.6 0.2 fusion.21
  439.8 1.0 fusion.80
  440.9 0.3 fusion.81
  441.1 1.8 fusion.75
  442.9 7.2 %fusion.76 = f32[2048,1024]{1,0:T(8,128)S(1)} fusion(f32[2048,128]{1,0:T(8,128)S(1)} %convolution_subtract_fusion.1, f32[128,1024]{1,0:T(8,128)S(1)} %fusion.75), kind=kOutput, calls=%fused_computation.121 | convolution fusion | flops 3221225472 | bytes 9961472 | tf_op jit(solution)/shard_map/dot_general | solution.py:84
  450.2 1.0 fusion.78
  451.2 1.0 convolution_subtract_fusion
  452.2 8.0 %subtract_bitcast_fusion = f32[1,2048,1,1024]{3,1,2,0:T(8,128)S(1)} fusion(f32[2048,1024]{1,0:T(8,128)S(1)} %bitcast.83, f32[2048,1024]{1,0:T(8,128)S(1)} %fusion.76, f32[2048,128]{1,0:T(8,128)S(1)} %convolution_subtract_fusion, f32[1024,128]{1,0:T(8,128)S(1)} %convolution_subtract_fusion.2), kind=kOutput, calls=%fused_computation.4 | convolution fusion | flops 3225419776 | bytes 26738688 | tf_op jit(solution)/shard_map/dot_general | solution.py:85
  460.2 16.1 %copy.18 = f32[1,2048,1,1024]{3,2,1,0:T(1,128)} copy(f32[1,2048,1,1024]{3,1,2,0:T(8,128)S(1)} %subtract_bitcast_fusion) | data formatting | bytes 16777216 | tf_op jit(solution)/shard_map/broadcast_in_dim | solution.py:90
  (21 shorter events, 0.2 us)
Async XLA Ops:
  6.5 105.1 %all-reduce.7.cloned.1.call-start = ((), (), s32[]{:S(2)}) async-start(), calls=%async_computation | async-start | bytes 8388608 | tf_op jit(solution)/shard_map/psum | solution.py:43
  12.3 206.3 %all-reduce.9.cloned.1.call-start = ((), (), s32[]{:S(2)}) async-start(), calls=%async_computation.1 | async-start | bytes 8388608 | tf_op jit(solution)/shard_map/psum | solution.py:43
  111.7 158.6 %all-reduce.11.cloned.1.call-start = ((), (), s32[]{:S(2)}) async-start(), calls=%async_computation.2 | async-start | bytes 131072 | tf_op jit(solution)/shard_map/psum | solution.py:56
  228.2 136.9 %all-reduce.13.cloned.1.call-start = ((), (), s32[]{:S(2)}) async-start(), calls=%async_computation.3 | async-start | bytes 2097152 | tf_op jit(solution)/shard_map/psum | solution.py:79
  305.7 109.4 %all-reduce.15.cloned.1.call-start = ((), (), s32[]{:S(2)}) async-start(), calls=%async_computation.4 | async-start | bytes 1310720 | tf_op jit(solution)/shard_map/psum | solution.py:56
  441.1 9.0 %copy-start = (f32[2048,128]{1,0:T(8,128)S(1)}, f32[2048,128]{1,0:T(8,128)}, u32[]{:S(2)}) copy-start(f32[2048,128]{1,0:T(8,128)} %all-reduce.13.cloned.1.call-done) | copy-start | bytes 3145732
  441.1 11.0 %slice-start = ((s8[8388608]{0:T(1024)(128)(4,1)}), s8[4194304]{0:T(1024)(128)(4,1)S(1)}, s32[]{:S(2)}) async-start(s8[8388608]{0:T(1024)(128)(4,1)} %bitcast.82), calls=%async_computation.5 | async-start | bytes 8388608
  442.9 9.3 %slice-start.1 = ((s8[8388608]{0:T(1024)(128)(4,1)}), s8[4194304]{0:T(1024)(128)(4,1)S(1)}, s32[]{:S(2)}) async-start(s8[8388608]{0:T(1024)(128)(4,1)} %bitcast.82), calls=%async_computation.6 | async-start | bytes 8388608
Sparse Core Ops, SparseCore 0:
  12.4 99.1 all-reduce.6
  114.9 103.6 all-reduce.8
  228.4 41.8 all-reduce.10
  305.8 59.2 all-reduce.12
  368.9 46.0 all-reduce.14
